TPU v7x, 32 devices: a whole 2x2x4 slice. The times are simulated.
32 devices in a mesh: seq: 16 (over z, y, x), head: 2 (over core).
Axes of the slice: x: 2, y: 2, z: 4, core: 2. Of those that a mesh axis runs over, the one named last changes fastest.
Arguments:
- queries: bfloat16 [2048, 2048], P('seq', 'head'), may hold values from -6 to 6
- keys: bfloat16 [2048, 512], P('seq', 'head'), may hold values from -6 to 6
- values: bfloat16 [2048, 512], P('seq', 'head'), may hold values from -6 to 6
- tile_mask: int32 [32, 32], replicated, may hold values from 0 to 1, as said below
- out_weight: bfloat16 [2048, 4096], P('head'), may hold values from -0.5 to 0.5
Outputs:
- mixed: bfloat16 [2048, 4096], P(('seq', 'head'))
Inputs may be any that keep to these rules, and one draw needn't show every extreme that they name: tile_mask[i, j] is 1 for i == j, 0 for j > i, and 0 or 1 below the diagonal.
All inputs are finite; a program needn't handle non-finite values.
Results may differ from a plain program's by a relative error of at most 0.01.
Values may be sent and summed in bfloat16 or wider, within the bound.
No kernel may reach another device: no remote copies, remote signals or barrier semaphores. Data moves between devices by JAX's collectives and lax.ppermute only.
A program may use at most 128 MiB of HBM per device.

v0:
```python
import math

import jax
import jax.numpy as jnp
from jax import lax
from jax.sharding import PartitionSpec as P

HD = 128
TILE = 64


MASK_FLOOR = -1e30


def per_device(queries, keys, values, tile_mask, out_weight):
    row_count = queries.shape[0]
    local_groups = keys.shape[1] // HD
    group = queries.shape[1] // HD // local_groups
    scale = 1.0 / math.sqrt(HD)
    seq_place = lax.axis_index("seq")
    query_index = seq_place * row_count + jnp.arange(row_count, dtype=jnp.int32)
    query_block = queries.reshape(row_count, local_groups, group, HD)
    query_tiles = query_index[::TILE] // TILE
    mask_rows = jnp.take(tile_mask, query_tiles, axis=0)

    def block_step(state, key_part, value_part, key_start):
        width = key_part.shape[0]
        key_index = key_start + jnp.arange(width, dtype=jnp.int32)
        tile_open = jnp.repeat(jnp.take(mask_rows, key_index // TILE, axis=1) > 0, TILE, axis=0)
        allowed = tile_open & (key_index[None, :] <= query_index[:, None])
        best, total, running = state
        allowed_wide = allowed[:, None, None, :]
        scores = (
            jnp.einsum(
                "qgrd,kgd->qgrk",
                query_block,
                key_part.reshape(width, local_groups, HD),
                preferred_element_type=jnp.float32,
            )
            * scale
        )
        masked = jnp.where(allowed_wide, scores, MASK_FLOOR)
        new_best = jnp.maximum(best, jnp.max(masked, axis=-1))
        weights = jnp.where(allowed_wide, jnp.exp(masked - new_best[..., None]), 0.0)
        rescale = jnp.exp(best - new_best)
        total = total * rescale + jnp.sum(weights, axis=-1)
        product = jnp.einsum(
            "qgrk,kgd->qgrd",
            weights.astype(jnp.bfloat16),
            value_part.reshape(width, local_groups, HD),
            preferred_element_type=jnp.float32,
        )
        running = running * rescale[..., None] + product
        return (new_best, total, running)

    initial = (
        jnp.full((row_count, local_groups, group), MASK_FLOOR, jnp.float32),
        jnp.zeros((row_count, local_groups, group), jnp.float32),
        jnp.zeros((row_count, local_groups, group, HD), jnp.float32),
    )
    carry = initial
    key_piece = lax.all_gather(keys, "seq", axis=0, tiled=True)
    value_piece = lax.all_gather(values, "seq", axis=0, tiled=True)
    width = key_piece.shape[0]
    block_size = math.gcd(width, 2048)
    count = width // block_size
    key_blocks = key_piece.reshape(count, block_size, key_piece.shape[1])
    value_blocks = value_piece.reshape(count, block_size, value_piece.shape[1])
    offsets = block_size * jnp.arange(count, dtype=jnp.int32)

    def advance(state, item):
        key_part, value_part, key_start = item
        return (block_step(state, key_part, value_part, key_start), None)

    carry, unused = lax.scan(advance, carry, (key_blocks, value_blocks, offsets))
    best, total, running = carry
    attended = (
        (running / total[..., None])
        .reshape(row_count, local_groups * group * HD)
        .astype(jnp.bfloat16)
    )
    return lax.psum_scatter(
        jnp.dot(attended, out_weight, preferred_element_type=jnp.float32).astype(jnp.bfloat16),
        "head",
        scatter_dimension=0,
        tiled=True,
    )


def solution(mesh):
    placed = (P("seq", "head"), P("seq", "head"), P("seq", "head"), P(), P("head", None))
    return jax.shard_map(
        per_device, mesh=mesh, in_specs=placed, out_specs=P(("seq", "head"), None), check_vma=False
    )
```

profile of v0, /device:TPU:0, one launch (start us, length us, event | category | flops | bytes accessed | tf_op | source)
XLA Modules:
  0.0 147.7 jit_solution(15410946941550882141)
XLA Ops:
  6.5 0.0 copy-start
  6.5 0.0 all-gather.3.cloned.1.call-start
  6.5 1.6 %copy.13 = bf16[128,256]{0,1:T(8,128)(2,1)} copy(bf16[128,256]{1,0:T(8,128)(2,1)} %param.6) | data formatting | bytes 131072 | tf_op args[1]
  8.1 0.0 all-gather.3.cloned.1.call-update
  8.1 0.0 all-gather.5.cloned.1.call-start
  8.2 0.7 all-gather.5.cloned.1.call-update
  8.9 0.0 reduce-scatter.2.cloned.1.call-start
  9.0 0.1 slice.3
  9.1 0.0 copy-done
  9.1 0.6 gather_fusion
  9.7 0.1 broadcast_select_fusion
  9.8 0.1 copy.10
  9.9 5.5 %gather_fusion.1 = s32[2048,2]{1,0:T(8,128)S(1)} fusion(s32[2,32]{0,1:T(8,128)S(1)} %copy.10, s32[2048]{0:T(1024)S(1)} %broadcast_clamp_fusion), kind=kCustom, calls=%fused_computation.1 | custom fusion | bytes 40960 | tf_op jit(solution)/shard_map/while/body/eval_jaxpr/jit(_take)/gather | solution.py:29
  15.3 0.3 fusion.13
  15.7 0.4 copy.11
  16.0 0.3 fusion.12
  16.3 0.5 copy.12
  16.7 1.1 reshape.123
  17.9 46.3 %all-gather.3.cloned.1.call-done = bf16[2048,256]{0,1:T(8,128)(2,1)} async-done(((bf16[128,256]{0,1:T(8,128)(2,1)}), bf16[2048,256]{0,1:T(8,128)(2,1)}) %all-gather.3.cloned.1.call-update) | async-done | bytes 1048592 | tf_op jit(solution)/shard_map/all_gather | solution.py:62
  64.2 2.7 %fusion = (f32[128,2,4]{0,2,1:T(4,128)S(1)}, f32[2,2048,128,4]{2,1,3,0:T(8,128)S(1)}) fusion(pred[128,2048]{0,1:T(8,128)(4,1)S(1)} %copy.12, bf16[2048,2,128,1]{0,2,3,1:T(8,128)(2,1)} %bitcast.47, bf16[128,2,4,128]{3,2,1,0:T(4,128)(2,1)S(1)} %reshape.123), kind=kOutput, calls=%fused_computation.4 | convolution fusion | flops 543161344 | bytes 9965568 | tf_op jit(solution)/shard_map/while/body/eval_jaxpr/qgrd,kgd->qgrk/dot_general | solution.py:34
  66.9 0.0 copy-start.1
  66.9 3.2 %copy-done.1 = f32[2,2048,128,4]{2,1,3,0:T(8,128)} copy-done((f32[2,2048,128,4]{2,1,3,0:T(8,128)}, f32[2,2048,128,4]{2,1,3,0:T(8,128)S(1)}, u32[]{:S(2)}) %copy-start.1) | copy-done | bytes 8388632
  70.1 2.0 %fusion.1 = f32[128,2,4]{0,2,1:T(4,128)S(1)} fusion(f32[2,2048,128,4]{2,1,3,0:T(8,128)S(1)} %get-tuple-element.26, f32[128,2,4]{0,2,1:T(4,128)S(1)} %broadcast_maximum_fusion, pred[128,2048]{0,1:T(8,128)(4,1)S(1)} %copy.12), kind=kLoop, calls=%fused_computation.5 | loop fusion | flops 10484736 | bytes 8658944 | tf_op jit(solution)/shard_map/while/body/eval_jaxpr/reduce_sum | solution.py:46
  72.2 48.9 %all-gather.5.cloned.1.call-done = bf16[2048,256]{1,0:T(8,128)(2,1)} async-done(((bf16[128,256]{1,0:T(8,128)(2,1)}), bf16[2048,256]{1,0:T(8,128)(2,1)}) %all-gather.5.cloned.1.call-update) | async-done | bytes 1048592 | tf_op jit(solution)/shard_map/all_gather | solution.py:63
  121.1 1.5 %copy.16 = bf16[2048,256]{0,1:T(8,128)(2,1)S(1)} copy(bf16[2048,256]{1,0:T(8,128)(2,1)} %all-gather.5.cloned.1.call-done) | data formatting | bytes 2097152 | tf_op jit(solution)/shard_map/all_gather | solution.py:63
  122.6 5.5 %fusion.17 = bf16[128,2,4,128]{0,3,2,1:T(8,128)(2,1)S(1)} fusion(bf16[2048,2,128,1]{0,2,3,1:T(8,128)(2,1)S(1)} %bitcast.48, f32[2,2048,128,4]{2,1,3,0:T(8,128)} %copy-done.1, f32[128,2,4]{0,2,1:T(4,128)S(1)} %broadcast_maximum_fusion, pred[128,2048]{0,1:T(8,128)(4,1)S(1)} %copy.12, f32[128,2,4]{0,2,1:T(4,128)S(1)} %get-tuple-element.24, ...), kind=kOutput, calls=%fused_computation.17 | convolution fusion | flops 547749888 | bytes 9973760 | tf_op jit(solution)/shard_map/while/body/eval_jaxpr/qgrk,kgd->qgrd/dot_general | solution.py:47
  128.1 5.6 %convolution_convert_fusion = bf16[128,4096]{1,0:T(8,128)(2,1)} fusion(bf16[128,1024]{0,1:T(8,128)(2,1)S(1)} %bitcast.49, bf16[1024,4096]{1,0:T(8,128)(2,1)} %param.9), kind=kOutput, calls=%fused_computation.7 | convolution fusion | flops 1074266112 | bytes 9699328 | tf_op jit(solution)/shard_map/dot_general | solution.py:83
  133.7 0.0 reduce-scatter.2.cloned.1.call-update
  133.8 7.4 %reduce-scatter.2.cloned.1.call-done = bf16[64,4096]{1,0:T(8,128)(2,1)} async-done(((bf16[128,4096]{1,0:T(8,128)(2,1)}), bf16[64,4096]{1,0:T(8,128)(2,1)}) %reduce-scatter.2.cloned.1.call-update) | async-done | bytes 524304 | tf_op jit(solution)/shard_map/reduce_scatter | solution.py:82
  (8 shorter events, 0.1 us)
Async XLA Ops:
  6.5 2.6 %copy-start = (s32[32,32]{1,0:T(8,128)S(1)}, s32[32,32]{1,0:T(8,128)}, u32[]{:S(2)}) copy-start(s32[32,32]{1,0:T(8,128)} %param.8) | copy-start | bytes 12292
  6.5 57.6 %all-gather.3.cloned.1.call-start = ((), (), s32[]{:S(2)}) async-start(), calls=%async_computation.1 | async-start | bytes 1114112 | tf_op jit(solution)/shard_map/all_gather | solution.py:62
  8.1 112.9 %all-gather.5.cloned.1.call-start = ((), (), s32[]{:S(2)}) async-start(), calls=%async_computation.2 | async-start | bytes 1114112 | tf_op jit(solution)/shard_map/all_gather | solution.py:63
  8.9 132.2 %reduce-scatter.2.cloned.1.call-start = ((), (), s32[]{:S(2)}) async-start(), calls=%async_computation.3 | async-start | bytes 1572864 | tf_op jit(solution)/shard_map/reduce_scatter | solution.py:82
  66.9 3.2 %copy-start.1 = (f32[2,2048,128,4]{2,1,3,0:T(8,128)}, f32[2,2048,128,4]{2,1,3,0:T(8,128)S(1)}, u32[]{:S(2)}) copy-start(f32[2,2048,128,4]{2,1,3,0:T(8,128)S(1)} %get-tuple-element.26) | copy-start | bytes 25165828
Sparse Core Ops, SparseCore 0:
  10.0 54.0 all-gather.2
  66.9 54.0 all-gather.4
  133.9 7.2 reduce-scatter.1
where the time goes:
time: 148 us
  waiting for transfers between devices  103 us (70%)
  local copies, waits for them, and re-layouts  14.4 us (10%)
  matrix products  13.9 us (9%)
  between operations  13.2 us (9%)
  other arithmetic  2.75 us (2%)
    all_gather x1, waiting for transfers between devices, per_device(): value_piece = lax.all_gather(values, 'seq', axis=0, tiled=True)  48.9 us
    all_gather x1, waiting for transfers between devices, per_device(): key_piece = lax.all_gather(keys, 'seq', axis=0, tiled=True)  46.3 us
    reduce_scatter x1, waiting for transfers between devices, per_device(): lax.psum_scatter(jnp.dot(attended, out_weight, preferred_element_type=jnp...  7.38 us
    dot_general x1, matrix products, per_device(): jnp.dot(attended, out_weight, preferred_element_type=jnp.float32)  5.64 us
    dot_general x1, matrix products, block_step(): jnp.einsum('qgrk,kgd->qgrd', weights.astype(jnp.bfloat16), value_part.res...  5.52 us
    gather x1, local copies, waits for them, and re-layouts, block_step(): jnp.take(mask_rows, key_index // TILE, axis=1) > 0  5.46 us
    unnamed x5, local copies, waits for them, and re-layouts  4.8 us
  transfers between devices with their start and end apart: 3, of which 3 were waited for; matrix products, arithmetic and copies ran while one was open for 9% of the time, Pallas kernels for 0%

commit v1 on v0

v1 whole, which is shorter than its diff:
```python
import functools
import math

import jax
import jax.numpy as jnp
from jax import lax
from jax.experimental import pallas as pl
from jax.experimental.pallas import tpu as pltpu
from jax.sharding import PartitionSpec as P


HD = 128
TILE = 64
FLOOR = -1e30
GRANT = 60 * 1024 * 1024
STAGE = 2048
BOTH = ("seq", "head")
VMEM = pl.BlockSpec(memory_space=pltpu.VMEM)
HBM = pl.BlockSpec(memory_space=pl.ANY)


class Plan:
    def __init__(self, mesh, local_groups, group, rows, tiles):
        self.S, self.H = mesh.shape["seq"], mesh.shape["head"]
        self.L, self.group, self.rows, self.tiles = local_groups, group, rows, tiles
        self.g = self.L * self.H
        self.X = self.g // 2
        self.A = self.S // (2 * self.g)
        assert self.g % 2 == 0 and self.S % (2 * self.g) == 0

    def place(self, a, y, j):
        return ((a * 2 + j // self.X) * 2 + y) * self.X + j % self.X

    def split(self, s):
        x, y, b, a = s % self.X, s // self.X % 2, s // (2 * self.X) % 2, s // (4 * self.X)
        return a, y, b * self.X + x

    def flat(self, a, y, j, h):
        return self.place(a, y, j) * self.H + h

    def out_pairs(self, k, t):
        return [
            (self.flat(a, y, j, h), self.flat(a + k, y, h * self.L + (j % self.L + t) % self.L, j // self.L))
            for a in range(self.A - k)
            for y in range(2)
            for j in range(self.g)
            for h in range(self.H)
        ]

    def back_pairs(self, t):
        return [(b, a) for a, b in self.out_pairs(0, t)]

    def side_pairs(self):
        return [
            (self.flat(a, 1 - y, j, h), self.flat(a, y, j, h))
            for a in range(self.A)
            for y in range(2)
            for j in range(self.g)
            for h in range(self.H)
        ]

    def head_pairs(self, u):
        return [((c + u) % self.H, c) for c in range(self.H)]

    def far(self):
        return sorted(range(1, self.A), key=lambda k: -k * (self.A - k))

    def block(self, s, c, span, t):
        k, side, u = span
        a, y, i = self.split(s)
        j = (c + u) % self.H * self.L + (i + self.L - t) % self.L
        return self.place(a - k, y + side - 2 * y * side, j)


def dot_nt(a, b):
    return lax.dot_general(a, b, (((1,), (1,)), ((), ())), preferred_element_type=jnp.float32)


def tile_bias(plan, mask, s, c, spans, t):
    L, R, T = plan.L, plan.rows, plan.tiles
    first = plan.block(s, c, (0, 0, 0), t) * (R // TILE)
    pick = jnp.where(
        lax.broadcasted_iota(jnp.int32, (8, T), 1) == lax.broadcasted_iota(jnp.int32, (8, T), 0) + first, 1.0, 0.0
    ).astype(jnp.bfloat16)
    rows = jnp.dot(pick, mask, preferred_element_type=jnp.float32).astype(jnp.bfloat16)
    tile_of = lax.broadcasted_iota(jnp.int32, (T, R), 1) // TILE
    row_of = lax.broadcasted_iota(jnp.int32, (T, R), 0)
    part = []
    for span in spans:
        for tt in range(L):
            base = plan.block(s, c, span, tt) * (R // TILE)
            part.append(jnp.where(row_of == tile_of + base, 1.0, 0.0).astype(jnp.bfloat16))
    seen = jnp.dot(rows, jnp.concatenate(part, axis=1), preferred_element_type=jnp.float32)
    return jnp.where(seen > 0.5, 0.0, FLOOR)


def score_scale():
    return math.log2(math.e) / math.sqrt(HD)


def attend_body(plan, spans, where, count, whole, mask_ref, *refs):
    L, G, R = plan.L, plan.group, plan.rows
    n = len(spans)
    q_refs, refs = refs[:L], refs[L:]
    kv_refs, refs = refs[:count], refs[count:]
    out_refs, refs = refs[:L], refs[L:]
    if not whole:
        top_refs, refs = refs[:L], refs[L:]
    s_ref, b_ref, k_ref, v_ref = refs
    s, c = lax.axis_index("seq"), lax.axis_index("head")
    scale = score_scale()
    mask = mask_ref[...]
    W = L * R
    rts = R // TILE
    for t in range(L):
        b_ref[t] = tile_bias(plan, mask, s, c, spans, t)
    for m, span in enumerate(spans):
        for t in range(L):
            index, row = where[span, t]
            at = slice(m * W + t * R, m * W + (t + 1) * R)
            k_ref[at, :] = kv_refs[index][row : row + R, :HD]
            v_ref[at, :HD] = kv_refs[index][row : row + R, HD:]
    v_ref[:, HD:] = jnp.ones((n * W, HD), jnp.bfloat16)
    late = lax.broadcasted_iota(jnp.int32, (R, R), 1) > lax.broadcasted_iota(jnp.int32, (R, R), 0)
    corner = jnp.where(late, FLOOR, 0.0)
    for t in range(L):
        for e in range(G):
            q = q_refs[t][:, e * HD : (e + 1) * HD]
            high = None
            for m in range(n):
                sc = dot_nt(q, k_ref[m * W : (m + 1) * W, :])
                b = b_ref[t, :rts, m * W : (m + 1) * W]
                sc = (sc.reshape(rts, TILE, W) + b.reshape(rts, 1, W)).reshape(R, W)
                for tt in range(L):
                    x = sc[:, tt * R : (tt + 1) * R]
                    if spans[m] == (0, 0, 0) and tt == t:
                        x = x + corner
                    s_ref[:, m * W + tt * R : m * W + (tt + 1) * R] = x
                    high = x if high is None else jnp.maximum(high, x)
            top = jnp.max(high, axis=1, keepdims=True)
            total = None
            for m in range(n):
                w = jnp.exp2((s_ref[:, m * W : (m + 1) * W] - top) * scale).astype(jnp.bfloat16)
                d = jnp.dot(w, v_ref[m * W : (m + 1) * W, :], preferred_element_type=jnp.float32)
                total = d if total is None else total + d
            at = slice(e * HD, (e + 1) * HD)
            if whole:
                out_refs[t][:, at] = (total[:, :HD] / total[:, HD:]).astype(jnp.bfloat16)
            else:
                out_refs[t][e * R : (e + 1) * R, :] = total
                top_refs[t][e * R : (e + 1) * R, :] = jnp.broadcast_to(top, (R, HD))


def attend_stage(plan, spans, mask, q, kv, whole):
    L, G, R = plan.L, plan.group, plan.rows
    arrays, where = [], {}
    for span in spans:
        for t in range(L):
            array, row = kv[span, t]
            index = next((n for n, x in enumerate(arrays) if x is array), len(arrays))
            if index == len(arrays):
                arrays.append(array)
            where[span, t] = index, row
    keys = len(spans) * L * R
    if whole:
        shapes = [jax.ShapeDtypeStruct((R, G * HD), jnp.bfloat16)] * L
    else:
        shapes = [jax.ShapeDtypeStruct((G * R, 2 * HD), jnp.float32)] * L
        shapes += [jax.ShapeDtypeStruct((G * R, HD), jnp.float32)] * L
    return pl.pallas_call(
        functools.partial(attend_body, plan, spans, where, len(arrays), whole),
        out_shape=shapes,
        in_specs=[VMEM] * (1 + L + len(arrays)),
        out_specs=[VMEM] * len(shapes),
        scratch_shapes=[
            pltpu.VMEM((R, keys), jnp.float32),
            pltpu.VMEM((L, 8, keys), jnp.float32),
            pltpu.VMEM((keys, HD), jnp.bfloat16),
            pltpu.VMEM((keys, 2 * HD), jnp.bfloat16),
        ],
        compiler_params=pltpu.CompilerParams(vmem_limit_bytes=8 << 20),
        cost_estimate=pl.CostEstimate(flops=2 * L * G * R * keys * 3 * HD, bytes_accessed=0, transcendentals=0),
        name="attend",
    )(mask, *q, *arrays)


def attend(plan, spans, mask, q, kv):
    L, G, R = plan.L, plan.group, plan.rows
    step = max(1, STAGE // (L * R))
    if len(spans) <= step:
        return attend_stage(plan, spans, mask, q, kv, True)
    parts = [attend_stage(plan, spans[n : n + step], mask, q, kv, False) for n in range(0, len(spans), step)]
    outs = []
    for t in range(L):
        top = functools.reduce(jnp.maximum, [p[L + t][:, :1] for p in parts])
        total = sum(p[t] * jnp.exp2((p[L + t][:, :1] - top) * score_scale()) for p in parts)
        o = (total[:, :HD] / total[:, HD:]).astype(jnp.bfloat16)
        outs.append(o.reshape(G, R, HD).transpose(1, 0, 2).reshape(R, G * HD))
    return outs


def hold_body(w_ref, out_ref, sem):
    copy = pltpu.make_async_copy(w_ref, out_ref, sem)
    copy.start()
    copy.wait()


def hold(w):
    size = w.size * w.dtype.itemsize
    return pl.pallas_call(
        hold_body,
        out_shape=jax.ShapeDtypeStruct(w.shape, w.dtype),
        in_specs=[HBM],
        out_specs=VMEM,
        scratch_shapes=[pltpu.SemaphoreType.DMA],
        compiler_params=pltpu.CompilerParams(vmem_limit_bytes=GRANT - size * 17 // 8),
        cost_estimate=pl.CostEstimate(flops=1 << 20, bytes_accessed=0, transcendentals=0),
        name="hold",
    )(w)


def project_body(plan, cols, w_ref, *refs):
    L, H, R = plan.L, plan.H, plan.rows
    a_refs, (send_ref, own_ref, sum_ref) = refs[:L], refs[L:]
    h = lax.axis_index("head")
    _, _, j = plan.split(lax.axis_index("seq"))
    depth = a_refs[0].shape[1]
    part = R // H
    for n in range(own_ref.shape[1] // cols):
        at = slice(n * cols, (n + 1) * cols)
        total = None
        for t in range(L):
            w = w_ref[pl.ds(pl.multiple_of((j + t) % L * depth, depth), depth), at]
            d = jnp.dot(a_refs[t][...], w, preferred_element_type=jnp.float32)
            total = d if total is None else total + d
        sum_ref[:, at] = total
        own_ref[:, at] = sum_ref[pl.ds(pl.multiple_of(h * part, part), part), at]
        for u in range(1, H):
            to = (h + u) % H
            send_ref[(u - 1) * part : u * part, at] = sum_ref[pl.ds(pl.multiple_of(to * part, part), part), at].astype(
                jnp.bfloat16
            )


def project(plan, pieces, w):
    H, R = plan.H, plan.rows
    depth, D = w.shape
    part = R // H
    return pl.pallas_call(
        functools.partial(project_body, plan, 512),
        out_shape=[
            jax.ShapeDtypeStruct(((H - 1) * part, D), jnp.bfloat16),
            jax.ShapeDtypeStruct((part, D), jnp.float32),
        ],
        in_specs=[VMEM] * (1 + len(pieces)),
        out_specs=[VMEM] * 2,
        scratch_shapes=[pltpu.VMEM((R, D), jnp.float32)],
        compiler_params=pltpu.CompilerParams(vmem_limit_bytes=6 << 20),
        cost_estimate=pl.CostEstimate(flops=2 * R * depth * D, bytes_accessed=0, transcendentals=0),
        name="project",
    )(w, *pieces)


def layer(plan, queries, keys, values, tile_mask, out_weight):
    L, H, R = plan.L, plan.H, plan.rows
    wide = plan.group * HD
    _, _, j = plan.split(lax.axis_index("seq"))

    kv_send, q_send = [], []
    for t in range(L):
        p = (j + t) % L
        k_p = lax.dynamic_slice(keys, (0, p * HD), (R, HD))
        v_p = lax.dynamic_slice(values, (0, p * HD), (R, HD))
        kv_send.append(jnp.concatenate([k_p, v_p], axis=1))
        q_send.append(lax.dynamic_slice(queries, (0, p * wide), (R, wide)))
    mask = tile_mask.astype(jnp.bfloat16)
    weight = hold(out_weight)

    kv = {}
    side = plan.side_pairs()
    own = {(k, t): lax.ppermute(kv_send[t], BOTH, plan.out_pairs(k, t)) for k in [0, *plan.far()] for t in range(L)}
    near = jnp.concatenate([own[0, t] for t in range(L)], axis=0)
    near_side = lax.ppermute(near, BOTH, side)
    q = [lax.ppermute(q_send[t], BOTH, plan.out_pairs(0, t)) for t in range(L)]
    for t in range(L):
        kv[(0, 0, 0), t] = near, t * R
        kv[(0, 1, 0), t] = near_side, t * R
    both = jnp.concatenate([near, near_side], axis=0)
    for u in range(1, H):
        got = lax.ppermute(both, "head", plan.head_pairs(u))
        for t in range(L):
            kv[(0, 0, u), t] = got, t * R
            kv[(0, 1, u), t] = got, (L + t) * R
    for k in plan.far():
        far = [own[k, t] for t in range(L)]
        far_side = [lax.ppermute(far[t], BOTH, side) for t in range(L)]
        for t in range(L):
            kv[(k, 0, 0), t] = far[t], 0
            kv[(k, 1, 0), t] = far_side[t], 0
        for n, block in enumerate((far, far_side)):
            both = jnp.concatenate(block, axis=0)
            for u in range(1, H):
                got = lax.ppermute(both, "head", plan.head_pairs(u))
                for t in range(L):
                    kv[(k, n, u), t] = got, t * R
    spans = [(k, n, u) for k in [0, *plan.far()] for n in range(2) for u in range(H)]
    outs = attend(plan, spans, mask, q, kv)
    pieces = [lax.ppermute(outs[t], BOTH, plan.back_pairs(t)) for t in range(L)]
    send, mine = project(plan, pieces, weight)
    part = R // H
    for u in range(1, H):
        got = lax.ppermute(send[(u - 1) * part : u * part], "head", [(c, (c + u) % H) for c in range(H)])
        mine = mine + got.astype(jnp.float32)
    return mine.astype(jnp.bfloat16)


def solution(mesh):
    def program(queries, keys, values, tile_mask, out_weight):
        groups = keys.shape[1] // mesh.shape["head"] // HD
        rows = queries.shape[0] // mesh.shape["seq"]
        plan = Plan(mesh, groups, queries.shape[1] // keys.shape[1], rows, tile_mask.shape[0])

        def body(*args):
            return layer(plan, *args)

        step = jax.shard_map(
            body,
            mesh=mesh,
            in_specs=(P("seq", "head"), P("seq", "head"), P("seq", "head"), P(), P("head", None)),
            out_specs=P(("seq", "head"), None),
            check_vma=False,
        )
        return step(queries, keys, values, tile_mask, out_weight)

    return program
```

time: 148 us -> 45.4 us (0.31)
  waiting for transfers between devices: 103 us -> 4.73 us
  starting transfers between devices: 0.08 us -> 28.1 us
  matrix products: 13.9 us -> 0 us
  between operations: 13.2 us -> 0.16 us
  local copies, waits for them, and re-layouts: 14.4 us -> 1.82 us
  Pallas kernels: 0 us -> 8.56 us
    all_gather x2 -> x0, waiting for transfers between devices: 95.2 us -> none  [the longest x1 48.9 us: per_device(): value_piece = lax.all_gather(values, 'seq', axis=0, tiled=True)]
    ppermute x0 -> x15, starting transfers between devices: none -> 28.1 us  [the longest x4 10.4 us: layer(): lax.ppermute(kv_send[t], BOTH, plan.out_pairs(k, t))]
    dot_general x3 -> x0, matrix products: 13.9 us -> none  [the longest x1 5.64 us: per_device(): jnp.dot(attended, out_weight, preferred_element_type=jnp.float32)]
    pallas_call x0 -> x3, Pallas kernels: none -> 8.56 us  [the longest x1 3.52 us: attend_stage(): pl.pallas_call(functools.partial(attend_body, plan, spans, where, len(arr...]
    reduce_scatter x1 -> x0, waiting for transfers between devices: 7.38 us -> none  [per_device(): lax.psum_scatter(jnp.dot(attended, out_weight, preferred_element_type=jnp...]
    gather x2 -> x0, local copies, waits for them, and re-layouts: 6.02 us -> none  [the longest x1 5.46 us: block_step(): jnp.take(mask_rows, key_index // TILE, axis=1) > 0]
    unnamed x5 -> x1, local copies, waits for them, and re-layouts: 4.8 us -> 0.01 us
    ppermute x0 -> x15, waiting for transfers between devices: none -> 4.73 us  [the longest x4 2.24 us: layer(): lax.ppermute(kv_send[t], BOTH, plan.out_pairs(k, t))]
  transfers between devices with their start and end apart: 3 -> 15, of which waited for: 3 -> 4; matrix products, arithmetic and copies ran while one was open for 9% -> 4% of each run, Pallas kernels for 0% -> 8%
where the time goes in v1:
time: 45.4 us; the launch traced here: 45 us
  starting transfers between devices  28.1 us (62%)
  Pallas kernels  8.56 us (19%)
  waiting for transfers between devices  4.73 us (10%)
  local copies, waits for them, and re-layouts  1.82 us (4%)
  other arithmetic  1.66 us (4%)
    ppermute x4, starting transfers between devices, layer(): lax.ppermute(kv_send[t], BOTH, plan.out_pairs(k, t))  10.4 us
    ppermute x3, starting transfers between devices, layer(): got = lax.ppermute(both, 'head', plan.head_pairs(u))  7.51 us
    pallas_call x1, Pallas kernels, attend_stage(): pl.pallas_call(functools.partial(attend_body, plan, spans, where, len(arr...  3.52 us
    pallas_call x1, Pallas kernels, hold(): pl.pallas_call(hold_body, out_shape=jax.ShapeDtypeStruct(w.shape, w.dtype...  3.39 us
    ppermute x1, starting transfers between devices, layer(): lax.ppermute(send[(u - 1) * part:u * part], 'head', [(c, (c + u) % H) for...  3.15 us
    ppermute x4, waiting for transfers between devices, layer(): lax.ppermute(kv_send[t], BOTH, plan.out_pairs(k, t))  2.24 us
    ppermute x2, starting transfers between devices, layer(): far_side = [lax.ppermute(far[t], BOTH, side) for t in range(L)]  2.09 us
    ppermute x1, starting transfers between devices, layer(): near_side = lax.ppermute(near, BOTH, side)  2.05 us
  transfers between devices with their start and end apart: 15, of which 4 were waited for; matrix products, arithmetic and copies ran while one was open for 4% of the time, Pallas kernels for 8%

profile of v1, /device:TPU:0, one launch (start us, length us, event | category | flops | bytes accessed | tf_op | source)
XLA Modules:
  0.0 45.0 jit_solution(1014005786285941122)
XLA Ops:
  0.0 0.8 %constant_dynamic-slice_fusion = (bf16[128,128]{1,0:T(8,128)(2,1)S(1)}, bf16[128,128]{1,0:T(8,128)(2,1)S(1)}, bf16[128,128]{1,0:T(8,128)(2,1)S(1)}, bf16[128,128]{1,0:T(8,128)(2,1)S(1)}) fusion(bf16[128,256]{1,0:T(8,128)(2,1)} %param.7, s32[]{:T(128)S(6)} %select_n.45, s32[]{:T(128)S(6)} %select_n.44, bf16[128,256]{1,0:T(8,128)(2,1)} %param.6), kind=kLoop, calls=%fused_computation.8 | loop fusion | bytes 262152 | tf_op jit(solution)/shard_map/dynamic_slice | solution.py:273
  0.8 0.7 %collective-permute-start.2 = (bf16[128,256]{1,0:T(8,128)(2,1)S(1)}, bf16[128,256]{1,0:T(8,128)(2,1)S(1)}, u32[]{:S(2)}, u32[]{:S(2)}) collective-permute-start(bf16[128,256]{1,0:T(8,128)(2,1)S(1)} %pad_maximum_fusion.3), channel_id=1, source_target_pairs={{0,0},{1,8},{2,2},{3,10},{8,1},{9,9},{10,3},{11,11},{4,4},{5,12},{... | collective-permute-start | bytes 196616 | tf_op jit(solution)/shard_map/ppermute | solution.py:281
  1.5 3.0 %collective-permute-start.3 = (bf16[128,256]{1,0:T(8,128)(2,1)S(1)}, bf16[128,256]{1,0:T(8,128)(2,1)S(1)}, u32[]{:S(2)}, u32[]{:S(2)}) collective-permute-start(bf16[128,256]{1,0:T(8,128)(2,1)S(1)} %pad_maximum_fusion.4), channel_id=1, source_target_pairs={{0,2},{1,10},{2,0},{3,8},{8,3},{9,11},{10,1},{11,9},{4,6},{5,14},{... | collective-permute-start | bytes 196616 | tf_op jit(solution)/shard_map/ppermute | solution.py:281
  4.6 0.0 collective-permute-done.2
  4.6 2.2 %collective-permute-done.3 = bf16[128,256]{1,0:T(8,128)(2,1)S(1)} collective-permute-done((bf16[128,256]{1,0:T(8,128)(2,1)S(1)}, bf16[128,256]{1,0:T(8,128)(2,1)S(1)}, u32[]{:S(2)}, u32[]{:S(2)}) %collective-permute-start.3) | collective-permute-done | bytes 65568 | tf_op jit(solution)/shard_map/ppermute | solution.py:281
  6.8 2.0 %collective-permute-start.4 = (bf16[256,256]{1,0:T(8,128)(2,1)S(1)}, bf16[256,256]{1,0:T(8,128)(2,1)S(1)}, u32[]{:S(2)}, u32[]{:S(2)}) collective-permute-start(bf16[256,256]{1,0:T(8,128)(2,1)S(1)} %constant_dynamic-update-slice_fusion.refs_2_), channel_id=1, source_target_pairs={{4,0},{5,1},{6,2},{7,3},{12,8},{13,9},{14,10},{15,11},{0,4},{1,5},... | collective-permute-start | bytes 393224 | tf_op jit(solution)/shard_map/ppermute | solution.py:283
  8.9 4.5 %collective-permute-start.6 = (bf16[128,256]{1,0:T(8,128)(2,1)S(1)}, bf16[128,256]{1,0:T(8,128)(2,1)S(1)}, u32[]{:S(2)}, u32[]{:S(2)}) collective-permute-start(bf16[128,256]{1,0:T(8,128)(2,1)S(1)} %pad_maximum_fusion.3), channel_id=1, source_target_pairs={{0,16},{1,24},{2,18},{3,26},{8,17},{9,25},{10,19},{11,27},{4,20},{... | collective-permute-start | bytes 196616 | tf_op jit(solution)/shard_map/ppermute | solution.py:281
  13.4 2.2 %collective-permute-start.7 = (bf16[128,256]{1,0:T(8,128)(2,1)S(1)}, bf16[128,256]{1,0:T(8,128)(2,1)S(1)}, u32[]{:S(2)}, u32[]{:S(2)}) collective-permute-start(bf16[128,256]{1,0:T(8,128)(2,1)S(1)} %pad_maximum_fusion.4), channel_id=1, source_target_pairs={{0,18},{1,26},{2,16},{3,24},{8,19},{9,27},{10,17},{11,25},{4,22},{... | collective-permute-start | bytes 196616 | tf_op jit(solution)/shard_map/ppermute | solution.py:281
  15.6 1.0 %constant_dynamic-slice_fusion.4 = (bf16[128,512]{1,0:T(8,128)(2,1)S(1)}, bf16[128,512]{1,0:T(8,128)(2,1)S(1)}) fusion(bf16[128,1024]{1,0:T(8,128)(2,1)} %param.5, s32[]{:T(128)S(6)} %select_n.43, s32[]{:T(128)S(6)} %select_n.41), kind=kLoop, calls=%fused_computation.12 | loop fusion | bytes 524296 | tf_op jit(solution)/shard_map/dynamic_slice | solution.py:275
  16.6 0.6 %collective-permute-start.1 = (bf16[128,512]{1,0:T(8,128)(2,1)S(1)}, bf16[128,512]{1,0:T(8,128)(2,1)S(1)}, u32[]{:S(2)}, u32[]{:S(2)}) collective-permute-start(bf16[128,512]{1,0:T(8,128)(2,1)S(1)} %get-tuple-element.13), channel_id=1, source_target_pairs={{0,2},{1,10},{2,0},{3,8},{8,3},{9,11},{10,1},{11,9},{4,6},{5,14},{... | collective-permute-start | bytes 393224 | tf_op jit(solution)/shard_map/ppermute | solution.py:284
  17.2 0.7 %collective-permute-start = (bf16[128,512]{1,0:T(8,128)(2,1)S(1)}, bf16[128,512]{1,0:T(8,128)(2,1)S(1)}, u32[]{:S(2)}, u32[]{:S(2)}) collective-permute-start(bf16[128,512]{1,0:T(8,128)(2,1)S(1)} %get-tuple-element.14), channel_id=1, source_target_pairs={{0,0},{1,8},{2,2},{3,10},{8,1},{9,9},{10,3},{11,11},{4,4},{5,12},{... | collective-permute-start | bytes 393224 | tf_op jit(solution)/shard_map/ppermute | solution.py:284
  17.9 0.0 collective-permute-done.6.refs_5_
  17.9 0.6 %collective-permute-start.9 = (bf16[128,256]{1,0:T(8,128)(2,1)S(1)}, bf16[128,256]{1,0:T(8,128)(2,1)S(1)}, u32[]{:S(2)}, u32[]{:S(2)}) collective-permute-start(bf16[128,256]{1,0:T(8,128)(2,1)S(1)} %collective-permute-done.6.refs_5_), channel_id=1, source_target_pairs={{4,0},{5,1},{6,2},{7,3},{12,8},{13,9},{14,10},{15,11},{0,4},{1,5},... | collective-permute-start | bytes 196616 | tf_op jit(solution)/shard_map/ppermute | solution.py:296
  18.5 0.0 collective-permute-done.7.refs_6_
  18.5 1.5 %collective-permute-start.10 = (bf16[128,256]{1,0:T(8,128)(2,1)S(1)}, bf16[128,256]{1,0:T(8,128)(2,1)S(1)}, u32[]{:S(2)}, u32[]{:S(2)}) collective-permute-start(bf16[128,256]{1,0:T(8,128)(2,1)S(1)} %collective-permute-done.7.refs_6_), channel_id=1, source_target_pairs={{4,0},{5,1},{6,2},{7,3},{12,8},{13,9},{14,10},{15,11},{0,4},{1,5},... | collective-permute-start | bytes 196616 | tf_op jit(solution)/shard_map/ppermute | solution.py:296
  20.0 0.0 collective-permute-done.4.refs_4_
  20.0 5.2 %collective-permute-start.5 = (bf16[512,256]{1,0:T(8,128)(2,1)S(1)}, bf16[512,256]{1,0:T(8,128)(2,1)S(1)}, u32[]{:S(2)}, u32[]{:S(2)}) collective-permute-start(bf16[512,256]{1,0:T(8,128)(2,1)S(1)} %pad_maximum_fusion), channel_id=1, source_target_pairs={{1,0},{0,1},{3,2},{2,3},{5,4},{4,5},{7,6},{6,7},{9,8},{8,9},{11,10... | collective-permute-start | bytes 786440 | tf_op jit(solution)/shard_map/ppermute | solution.py:290
  25.2 0.0 collective-permute-done.9.refs_8_
  25.3 1.5 %collective-permute-start.8 = (bf16[256,256]{1,0:T(8,128)(2,1)S(1)}, bf16[256,256]{1,0:T(8,128)(2,1)S(1)}, u32[]{:S(2)}, u32[]{:S(2)}) collective-permute-start(bf16[256,256]{1,0:T(8,128)(2,1)S(1)} %pad_maximum_fusion.1), channel_id=1, source_target_pairs={{1,0},{0,1},{3,2},{2,3},{5,4},{4,5},{7,6},{6,7},{9,8},{8,9},{11,10... | collective-permute-start | bytes 393224 | tf_op jit(solution)/shard_map/ppermute | solution.py:303
  26.8 0.0 collective-permute-done.10.refs_9_
  26.8 0.8 %collective-permute-start.11 = (bf16[256,256]{1,0:T(8,128)(2,1)S(1)}, bf16[256,256]{1,0:T(8,128)(2,1)S(1)}, u32[]{:S(2)}, u32[]{:S(2)}) collective-permute-start(bf16[256,256]{1,0:T(8,128)(2,1)S(1)} %pad_maximum_fusion.2), channel_id=1, source_target_pairs={{1,0},{0,1},{3,2},{2,3},{5,4},{4,5},{7,6},{6,7},{9,8},{8,9},{11,10... | collective-permute-start | bytes 393224 | tf_op jit(solution)/shard_map/ppermute | solution.py:303
  27.6 0.7 %convert_element_type.9.mask_ref = bf16[32,32]{1,0:T(8,128)(2,1)S(1)} convert(s32[32,32]{1,0:T(8,128)} %param.8) | non-fusion elementwise | flops 1024 | bytes 6144 | tf_op jit(solution)/shard_map/convert_element_type | solution.py:276
  28.3 0.0 collective-permute-done.1.refs_1_
  28.3 0.0 collective-permute-done.refs_0_
  28.3 0.0 collective-permute-done.8.refs_7_
  28.3 0.2 collective-permute-done.11.refs_10_
  28.6 0.0 collective-permute-done.5.refs_3_
  28.6 3.5 %attend.1 = (bf16[128,512]{1,0:T(8,128)(2,1)S(1)}, bf16[128,512]{1,0:T(8,128)(2,1)S(1)}) custom-call(bf16[32,32]{1,0:T(8,128)(2,1)S(1)} %convert_element_type.9.mask_ref, bf16[128,512]{1,0:T(8,128)(2,1)S(1)} %collective-permute-done.refs_0_, bf16[128,512]{1,0:T(8,128)(2,1)S(1)} %collective-permute-done.1.refs_1_, ...), custom_call_target="tpu_custom_call" | custom-call | flops 1610612736 | tf_op jit(solution)/shard_map/attend/pallas_call | solution.py:170
  32.1 0.7 %collective-permute-start.12 = (bf16[128,512]{1,0:T(8,128)(2,1)S(1)}, bf16[128,512]{1,0:T(8,128)(2,1)S(1)}, u32[]{:S(2)}, u32[]{:S(2)}) collective-permute-start(bf16[128,512]{1,0:T(8,128)(2,1)S(1)} %get-tuple-element.9), channel_id=1, source_target_pairs={{0,0},{8,1},{2,2},{10,3},{1,8},{9,9},{3,10},{11,11},{4,4},{12,5},{... | collective-permute-start | bytes 393224 | tf_op jit(solution)/shard_map/ppermute | solution.py:308
  32.8 0.9 %collective-permute-start.13 = (bf16[128,512]{1,0:T(8,128)(2,1)S(1)}, bf16[128,512]{1,0:T(8,128)(2,1)S(1)}, u32[]{:S(2)}, u32[]{:S(2)}) collective-permute-start(bf16[128,512]{1,0:T(8,128)(2,1)S(1)} %get-tuple-element.10), channel_id=1, source_target_pairs={{2,0},{10,1},{0,2},{8,3},{3,8},{11,9},{1,10},{9,11},{6,4},{14,5},{... | collective-permute-start | bytes 393224 | tf_op jit(solution)/shard_map/ppermute | solution.py:308
  33.7 3.4 %hold.1.w_ref = bf16[1024,4096]{1,0:T(8,128)(2,1)S(1)} custom-call(bf16[1024,4096]{1,0:T(8,128)(2,1)} %w_ref.1), custom_call_target="tpu_custom_call" | custom-call | flops 1048576 | tf_op jit(solution)/shard_map/hold/pallas_call | solution.py:210
  37.1 0.0 collective-permute-done.12.refs_0_
  37.1 0.7 %collective-permute-done.13.refs_1_ = bf16[128,512]{1,0:T(8,128)(2,1)S(1)} collective-permute-done((bf16[128,512]{1,0:T(8,128)(2,1)S(1)}, bf16[128,512]{1,0:T(8,128)(2,1)S(1)}, u32[]{:S(2)}, u32[]{:S(2)}) %collective-permute-start.13) | collective-permute-done | bytes 131104 | tf_op jit(solution)/shard_map/ppermute | solution.py:308
  37.8 1.7 %project.1 = (bf16[64,4096]{1,0:T(8,128)(2,1)S(1)}, f32[64,4096]{1,0:T(8,128)S(1)}) custom-call(bf16[1024,4096]{1,0:T(8,128)(2,1)S(1)} %hold.1.w_ref, bf16[128,512]{1,0:T(8,128)(2,1)S(1)} %collective-permute-done.12.refs_0_, bf16[128,512]{1,0:T(8,128)(2,1)S(1)} %collective-permute-done.13.refs_1_), custom_call_target="tpu_custom_call" | custom-call | flops 1073741824 | tf_op jit(solution)/shard_map/project/pallas_call | solution.py:249
  39.5 3.2 %collective-permute-start.14 = (bf16[64,4096]{1,0:T(8,128)(2,1)S(1)}, bf16[64,4096]{1,0:T(8,128)(2,1)S(1)}, u32[]{:S(2)}, u32[]{:S(2)}) collective-permute-start(bf16[64,4096]{1,0:T(8,128)(2,1)S(1)} %get-tuple-element.12), channel_id=1, source_target_pairs={{0,1},{1,0},{2,3},{3,2},{4,5},{5,4},{6,7},{7,6},{8,9},{9,8},{10,11... | collective-permute-start | bytes 1572872 | tf_op jit(solution)/shard_map/ppermute | solution.py:312
  42.6 1.5 %collective-permute-done.14 = bf16[64,4096]{1,0:T(8,128)(2,1)S(1)} collective-permute-done((bf16[64,4096]{1,0:T(8,128)(2,1)S(1)}, bf16[64,4096]{1,0:T(8,128)(2,1)S(1)}, u32[]{:S(2)}, u32[]{:S(2)}) %collective-permute-start.14) | collective-permute-done | bytes 524320 | tf_op jit(solution)/shard_map/ppermute | solution.py:312
  44.1 0.9 %add_convert_fusion = bf16[64,4096]{1,0:T(8,128)(2,1)} fusion(f32[64,4096]{1,0:T(8,128)S(1)} %get-tuple-element.11, bf16[64,4096]{1,0:T(8,128)(2,1)S(1)} %collective-permute-done.14), kind=kLoop, calls=%fused_computation | loop fusion | flops 786432 | bytes 2097152 | tf_op jit(solution)/shard_map/convert_element_type | solution.py:314
  (7 shorter events, 0.1 us)
Async XLA Ops:
  0.8 3.7 %collective-permute-start.2 = (bf16[128,256]{1,0:T(8,128)(2,1)S(1)}, bf16[128,256]{1,0:T(8,128)(2,1)S(1)}, u32[]{:S(2)}, u32[]{:S(2)}) collective-permute-start(bf16[128,256]{1,0:T(8,128)(2,1)S(1)} %pad_maximum_fusion.3), channel_id=1, source_target_pairs={{0,0},{1,8},{2,2},{3,10},{8,1},{9,9},{10,3},{11,11},{4,4},{5,12},{... | collective-permute-start | bytes 196616 | tf_op jit(solution)/shard_map/ppermute | solution.py:281
  1.5 5.3 %collective-permute-start.3 = (bf16[128,256]{1,0:T(8,128)(2,1)S(1)}, bf16[128,256]{1,0:T(8,128)(2,1)S(1)}, u32[]{:S(2)}, u32[]{:S(2)}) collective-permute-start(bf16[128,256]{1,0:T(8,128)(2,1)S(1)} %pad_maximum_fusion.4), channel_id=1, source_target_pairs={{0,2},{1,10},{2,0},{3,8},{8,3},{9,11},{10,1},{11,9},{4,6},{5,14},{... | collective-permute-start | bytes 196616 | tf_op jit(solution)/shard_map/ppermute | solution.py:281
  6.8 13.2 %collective-permute-start.4 = (bf16[256,256]{1,0:T(8,128)(2,1)S(1)}, bf16[256,256]{1,0:T(8,128)(2,1)S(1)}, u32[]{:S(2)}, u32[]{:S(2)}) collective-permute-start(bf16[256,256]{1,0:T(8,128)(2,1)S(1)} %constant_dynamic-update-slice_fusion.refs_2_), channel_id=1, source_target_pairs={{4,0},{5,1},{6,2},{7,3},{12,8},{13,9},{14,10},{15,11},{0,4},{1,5},... | collective-permute-start | bytes 393224 | tf_op jit(solution)/shard_map/ppermute | solution.py:283
  8.9 9.0 %collective-permute-start.6 = (bf16[128,256]{1,0:T(8,128)(2,1)S(1)}, bf16[128,256]{1,0:T(8,128)(2,1)S(1)}, u32[]{:S(2)}, u32[]{:S(2)}) collective-permute-start(bf16[128,256]{1,0:T(8,128)(2,1)S(1)} %pad_maximum_fusion.3), channel_id=1, source_target_pairs={{0,16},{1,24},{2,18},{3,26},{8,17},{9,25},{10,19},{11,27},{4,20},{... | collective-permute-start | bytes 196616 | tf_op jit(solution)/shard_map/ppermute | solution.py:281
  13.4 5.1 %collective-permute-start.7 = (bf16[128,256]{1,0:T(8,128)(2,1)S(1)}, bf16[128,256]{1,0:T(8,128)(2,1)S(1)}, u32[]{:S(2)}, u32[]{:S(2)}) collective-permute-start(bf16[128,256]{1,0:T(8,128)(2,1)S(1)} %pad_maximum_fusion.4), channel_id=1, source_target_pairs={{0,18},{1,26},{2,16},{3,24},{8,19},{9,27},{10,17},{11,25},{4,22},{... | collective-permute-start | bytes 196616 | tf_op jit(solution)/shard_map/ppermute | solution.py:281
  16.6 11.7 %collective-permute-start.1 = (bf16[128,512]{1,0:T(8,128)(2,1)S(1)}, bf16[128,512]{1,0:T(8,128)(2,1)S(1)}, u32[]{:S(2)}, u32[]{:S(2)}) collective-permute-start(bf16[128,512]{1,0:T(8,128)(2,1)S(1)} %get-tuple-element.13), channel_id=1, source_target_pairs={{0,2},{1,10},{2,0},{3,8},{8,3},{9,11},{10,1},{11,9},{4,6},{5,14},{... | collective-permute-start | bytes 393224 | tf_op jit(solution)/shard_map/ppermute | solution.py:284
  17.2 11.1 %collective-permute-start = (bf16[128,512]{1,0:T(8,128)(2,1)S(1)}, bf16[128,512]{1,0:T(8,128)(2,1)S(1)}, u32[]{:S(2)}, u32[]{:S(2)}) collective-permute-start(bf16[128,512]{1,0:T(8,128)(2,1)S(1)} %get-tuple-element.14), channel_id=1, source_target_pairs={{0,0},{1,8},{2,2},{3,10},{8,1},{9,9},{10,3},{11,11},{4,4},{5,12},{... | collective-permute-start | bytes 393224 | tf_op jit(solution)/shard_map/ppermute | solution.py:284
  17.9 7.4 %collective-permute-start.9 = (bf16[128,256]{1,0:T(8,128)(2,1)S(1)}, bf16[128,256]{1,0:T(8,128)(2,1)S(1)}, u32[]{:S(2)}, u32[]{:S(2)}) collective-permute-start(bf16[128,256]{1,0:T(8,128)(2,1)S(1)} %collective-permute-done.6.refs_5_), channel_id=1, source_target_pairs={{4,0},{5,1},{6,2},{7,3},{12,8},{13,9},{14,10},{15,11},{0,4},{1,5},... | collective-permute-start | bytes 196616 | tf_op jit(solution)/shard_map/ppermute | solution.py:296
  18.5 8.3 %collective-permute-start.10 = (bf16[128,256]{1,0:T(8,128)(2,1)S(1)}, bf16[128,256]{1,0:T(8,128)(2,1)S(1)}, u32[]{:S(2)}, u32[]{:S(2)}) collective-permute-start(bf16[128,256]{1,0:T(8,128)(2,1)S(1)} %collective-permute-done.7.refs_6_), channel_id=1, source_target_pairs={{4,0},{5,1},{6,2},{7,3},{12,8},{13,9},{14,10},{15,11},{0,4},{1,5},... | collective-permute-start | bytes 196616 | tf_op jit(solution)/shard_map/ppermute | solution.py:296
  20.0 8.5 %collective-permute-start.5 = (bf16[512,256]{1,0:T(8,128)(2,1)S(1)}, bf16[512,256]{1,0:T(8,128)(2,1)S(1)}, u32[]{:S(2)}, u32[]{:S(2)}) collective-permute-start(bf16[512,256]{1,0:T(8,128)(2,1)S(1)} %pad_maximum_fusion), channel_id=1, source_target_pairs={{1,0},{0,1},{3,2},{2,3},{5,4},{4,5},{7,6},{6,7},{9,8},{8,9},{11,10... | collective-permute-start | bytes 786440 | tf_op jit(solution)/shard_map/ppermute | solution.py:290
  25.3 3.0 %collective-permute-start.8 = (bf16[256,256]{1,0:T(8,128)(2,1)S(1)}, bf16[256,256]{1,0:T(8,128)(2,1)S(1)}, u32[]{:S(2)}, u32[]{:S(2)}) collective-permute-start(bf16[256,256]{1,0:T(8,128)(2,1)S(1)} %pad_maximum_fusion.1), channel_id=1, source_target_pairs={{1,0},{0,1},{3,2},{2,3},{5,4},{4,5},{7,6},{6,7},{9,8},{8,9},{11,10... | collective-permute-start | bytes 393224 | tf_op jit(solution)/shard_map/ppermute | solution.py:303
  26.8 1.8 %collective-permute-start.11 = (bf16[256,256]{1,0:T(8,128)(2,1)S(1)}, bf16[256,256]{1,0:T(8,128)(2,1)S(1)}, u32[]{:S(2)}, u32[]{:S(2)}) collective-permute-start(bf16[256,256]{1,0:T(8,128)(2,1)S(1)} %pad_maximum_fusion.2), channel_id=1, source_target_pairs={{1,0},{0,1},{3,2},{2,3},{5,4},{4,5},{7,6},{6,7},{9,8},{8,9},{11,10... | collective-permute-start | bytes 393224 | tf_op jit(solution)/shard_map/ppermute | solution.py:303
  32.1 5.0 %collective-permute-start.12 = (bf16[128,512]{1,0:T(8,128)(2,1)S(1)}, bf16[128,512]{1,0:T(8,128)(2,1)S(1)}, u32[]{:S(2)}, u32[]{:S(2)}) collective-permute-start(bf16[128,512]{1,0:T(8,128)(2,1)S(1)} %get-tuple-element.9), channel_id=1, source_target_pairs={{0,0},{8,1},{2,2},{10,3},{1,8},{9,9},{3,10},{11,11},{4,4},{12,5},{... | collective-permute-start | bytes 393224 | tf_op jit(solution)/shard_map/ppermute | solution.py:308
  32.8 5.0 %collective-permute-start.13 = (bf16[128,512]{1,0:T(8,128)(2,1)S(1)}, bf16[128,512]{1,0:T(8,128)(2,1)S(1)}, u32[]{:S(2)}, u32[]{:S(2)}) collective-permute-start(bf16[128,512]{1,0:T(8,128)(2,1)S(1)} %get-tuple-element.10), channel_id=1, source_target_pairs={{2,0},{10,1},{0,2},{8,3},{3,8},{11,9},{1,10},{9,11},{6,4},{14,5},{... | collective-permute-start | bytes 393224 | tf_op jit(solution)/shard_map/ppermute | solution.py:308
  39.5 4.7 %collective-permute-start.14 = (bf16[64,4096]{1,0:T(8,128)(2,1)S(1)}, bf16[64,4096]{1,0:T(8,128)(2,1)S(1)}, u32[]{:S(2)}, u32[]{:S(2)}) collective-permute-start(bf16[64,4096]{1,0:T(8,128)(2,1)S(1)} %get-tuple-element.12), channel_id=1, source_target_pairs={{0,1},{1,0},{2,3},{3,2},{4,5},{5,4},{6,7},{7,6},{8,9},{9,8},{10,11... | collective-permute-start | bytes 1572872 | tf_op jit(solution)/shard_map/ppermute | solution.py:312

commit v2 on v1

v2 whole, which is shorter than its diff:
```python
import functools
import math

import jax
import jax.numpy as jnp
from jax import lax
from jax.experimental import pallas as pl
from jax.experimental.pallas import tpu as pltpu
from jax.sharding import PartitionSpec as P


HD = 128
TILE = 64
FLOOR = -1e30
GRANT = 60 * 1024 * 1024
STAGE = 2048
BOTH = ("seq", "head")
VMEM = pl.BlockSpec(memory_space=pltpu.VMEM)
HBM = pl.BlockSpec(memory_space=pl.ANY)


class Plan:
    def __init__(self, mesh, local_groups, group, rows, tiles):
        self.S, self.H = mesh.shape["seq"], mesh.shape["head"]
        self.L, self.group, self.rows, self.tiles = local_groups, group, rows, tiles
        self.g = self.L * self.H
        self.X = self.g // 2
        self.A = self.S // (2 * self.g)
        assert self.g % 2 == 0 and self.S % (2 * self.g) == 0

    def place(self, a, y, j):
        return ((a * 2 + j // self.X) * 2 + y) * self.X + j % self.X

    def split(self, s):
        x, y, b, a = s % self.X, s // self.X % 2, s // (2 * self.X) % 2, s // (4 * self.X)
        return a, y, b * self.X + x

    def flat(self, a, y, j, h):
        return self.place(a, y, j) * self.H + h

    def out_pairs(self, k, t):
        return [
            (self.flat(a, y, j, h), self.flat(a + k, y, h * self.L + (j % self.L + t) % self.L, j // self.L))
            for a in range(self.A - k)
            for y in range(2)
            for j in range(self.g)
            for h in range(self.H)
        ]

    def back_pairs(self, t):
        return [(b, a) for a, b in self.out_pairs(0, t)]

    def side_pairs(self):
        return [
            (self.flat(a, 1 - y, j, h), self.flat(a, y, j, h))
            for a in range(self.A)
            for y in range(2)
            for j in range(self.g)
            for h in range(self.H)
        ]

    def head_pairs(self, u):
        return [((c + u) % self.H, c) for c in range(self.H)]

    def far(self):
        return sorted(range(1, self.A), key=lambda k: -k * (self.A - k))

    def block(self, s, c, span, t):
        k, side, u = span
        a, y, i = self.split(s)
        j = (c + u) % self.H * self.L + (i + self.L - t) % self.L
        return self.place(a - k, y + side - 2 * y * side, j)


def dot_nt(a, b):
    return lax.dot_general(a, b, (((1,), (1,)), ((), ())), preferred_element_type=jnp.float32)


def tile_bias(plan, mask, s, c, spans, t):
    L, R, T = plan.L, plan.rows, plan.tiles
    first = plan.block(s, c, (0, 0, 0), t) * (R // TILE)
    pick = jnp.where(
        lax.broadcasted_iota(jnp.int32, (8, T), 1) == lax.broadcasted_iota(jnp.int32, (8, T), 0) + first, 1.0, 0.0
    ).astype(jnp.bfloat16)
    rows = jnp.dot(pick, mask, preferred_element_type=jnp.float32).astype(jnp.bfloat16)
    tile_of = lax.broadcasted_iota(jnp.int32, (T, R), 1) // TILE
    row_of = lax.broadcasted_iota(jnp.int32, (T, R), 0)
    part = []
    for span in spans:
        for tt in range(L):
            base = plan.block(s, c, span, tt) * (R // TILE)
            part.append(jnp.where(row_of == tile_of + base, 1.0, 0.0).astype(jnp.bfloat16))
    seen = jnp.dot(rows, jnp.concatenate(part, axis=1), preferred_element_type=jnp.float32)
    return jnp.where(seen > 0.5, 0.0, FLOOR)


def score_scale():
    return math.log2(math.e) / math.sqrt(HD)


def fill_keys(plan, spans, where, kv_refs, k_ref, v_ref):
    L, R = plan.L, plan.rows
    for m, span in enumerate(spans):
        for t in range(L):
            index, row = where[span, t]
            at = slice((m * L + t) * R, (m * L + t + 1) * R)
            k_ref[at, :] = kv_refs[index][row : row + R, :HD]
            v_ref[at, :HD] = kv_refs[index][row : row + R, HD:]
    v_ref[:, HD:] = jnp.ones((v_ref.shape[0], HD), jnp.bfloat16)


def attend_piece(plan, spans, t, s, c, mask, q_ref, k_ref, v_ref, s_ref, b_ref, write):
    L, G, R = plan.L, plan.group, plan.rows
    n, W, rts = len(spans), L * R, R // TILE
    scale = score_scale()
    b_ref[...] = tile_bias(plan, mask, s, c, spans, t)
    late = lax.broadcasted_iota(jnp.int32, (R, R), 1) > lax.broadcasted_iota(jnp.int32, (R, R), 0)
    corner = jnp.where(late, FLOOR, 0.0)
    for e in range(G):
        q = q_ref[:, (2 + e) * HD : (3 + e) * HD]
        high = None
        for m in range(n):
            sc = dot_nt(q, k_ref[m * W : (m + 1) * W, :])
            b = b_ref[:rts, m * W : (m + 1) * W]
            sc = (sc.reshape(rts, TILE, W) + b.reshape(rts, 1, W)).reshape(R, W)
            for tt in range(L):
                x = sc[:, tt * R : (tt + 1) * R]
                if spans[m] == (0, 0, 0) and tt == t:
                    x = x + corner
                s_ref[:, m * W + tt * R : m * W + (tt + 1) * R] = x
                high = x if high is None else jnp.maximum(high, x)
        top = jnp.max(high, axis=1, keepdims=True)
        total = None
        for m in range(n):
            w = jnp.exp2((s_ref[:, m * W : (m + 1) * W] - top) * scale).astype(jnp.bfloat16)
            d = jnp.dot(w, v_ref[m * W : (m + 1) * W, :], preferred_element_type=jnp.float32)
            total = d if total is None else total + d
        write(e, total, top)


def index_of(plan, spans, kv):
    arrays, where = [], {}
    for span in spans:
        for t in range(plan.L):
            array, row = kv[span, t]
            index = next((n for n, x in enumerate(arrays) if x is array), len(arrays))
            if index == len(arrays):
                arrays.append(array)
            where[span, t] = index, row
    return arrays, where


def stage_body(plan, spans, where, count, mask_ref, *refs):
    L, R = plan.L, plan.rows
    q_refs, refs = refs[:L], refs[L:]
    kv_refs, refs = refs[:count], refs[count:]
    out_refs, top_refs, (s_ref, b_ref, k_ref, v_ref) = refs[:L], refs[L : 2 * L], refs[2 * L :]
    s, c = lax.axis_index("seq"), lax.axis_index("head")
    fill_keys(plan, spans, where, kv_refs, k_ref, v_ref)
    for t in range(L):

        def write(e, total, top, t=t):
            out_refs[t][e * R : (e + 1) * R, :] = total
            top_refs[t][e * R : (e + 1) * R, :] = jnp.broadcast_to(top, (R, HD))

        attend_piece(plan, spans, t, s, c, mask_ref[...], q_refs[t], k_ref, v_ref, s_ref, b_ref, write)


def attend_stage(plan, spans, mask, q, kv):
    L, G, R = plan.L, plan.group, plan.rows
    arrays, where = index_of(plan, spans, kv)
    keys = len(spans) * L * R
    shapes = [jax.ShapeDtypeStruct((G * R, 2 * HD), jnp.float32)] * L
    shapes += [jax.ShapeDtypeStruct((G * R, HD), jnp.float32)] * L
    return pl.pallas_call(
        functools.partial(stage_body, plan, spans, where, len(arrays)),
        out_shape=shapes,
        in_specs=[VMEM] * (1 + L + len(arrays)),
        out_specs=[VMEM] * len(shapes),
        scratch_shapes=[
            pltpu.VMEM((R, keys), jnp.float32),
            pltpu.VMEM((8, keys), jnp.float32),
            pltpu.VMEM((keys, HD), jnp.bfloat16),
            pltpu.VMEM((keys, 2 * HD), jnp.bfloat16),
        ],
        compiler_params=pltpu.CompilerParams(vmem_limit_bytes=12 << 20),
        name="stage",
    )(mask, *q, *arrays)


def piece_body(plan, spans, t, where, count, mask_ref, q_ref, *refs):
    kv_refs, refs = refs[:count], refs[count:]
    if where is None:
        k_ref, v_ref = kv_refs
        out_ref, s_ref, b_ref = refs
    else:
        out_ref, k_ref, v_ref, s_ref, b_ref = refs
    s, c = lax.axis_index("seq"), lax.axis_index("head")
    if where is not None:
        fill_keys(plan, spans, where, kv_refs, k_ref, v_ref)

    def write(e, total, top):
        out_ref[:, e * HD : (e + 1) * HD] = (total[:, :HD] / total[:, HD:]).astype(jnp.bfloat16)

    attend_piece(plan, spans, t, s, c, mask_ref[...], q_ref, k_ref, v_ref, s_ref, b_ref, write)


def attend_one(plan, spans, t, mask, q, kv, where):
    L, G, R = plan.L, plan.group, plan.rows
    keys = len(spans) * L * R
    shapes = [jax.ShapeDtypeStruct((R, G * HD), jnp.bfloat16)]
    if where is not None:
        shapes += [jax.ShapeDtypeStruct((keys, HD), jnp.bfloat16), jax.ShapeDtypeStruct((keys, 2 * HD), jnp.bfloat16)]
    return pl.pallas_call(
        functools.partial(piece_body, plan, spans, t, where, len(kv)),
        out_shape=shapes,
        in_specs=[VMEM] * (2 + len(kv)),
        out_specs=[VMEM] * len(shapes),
        scratch_shapes=[pltpu.VMEM((R, keys), jnp.float32), pltpu.VMEM((8, keys), jnp.float32)],
        compiler_params=pltpu.CompilerParams(vmem_limit_bytes=6 << 20),
        cost_estimate=pl.CostEstimate(flops=2 * G * R * keys * 3 * HD, bytes_accessed=0, transcendentals=0),
    )(mask, q, *kv)


def attend_staged(plan, spans, mask, q, kv):
    L, G, R = plan.L, plan.group, plan.rows
    step = max(1, STAGE // (L * R))
    parts = [attend_stage(plan, spans[n : n + step], mask, q, kv) for n in range(0, len(spans), step)]
    outs = []
    for t in range(L):
        top = functools.reduce(jnp.maximum, [p[L + t][:, :1] for p in parts])
        total = sum(p[t] * jnp.exp2((p[L + t][:, :1] - top) * score_scale()) for p in parts)
        o = (total[:, :HD] / total[:, HD:]).astype(jnp.bfloat16)
        outs.append(o.reshape(G, R, HD).transpose(1, 0, 2).reshape(R, G * HD))
    return outs


def hold_body(plan, t, w_ref, *refs):
    _, _, j = plan.split(lax.axis_index("seq"))
    if t == 0:
        mask_ref, out_ref, open_ref, raw_ref, sem = refs
    else:
        out_ref, sem = refs
    depth = out_ref.shape[0]
    here = pl.ds(pl.multiple_of((j + t) % plan.L * depth, depth), depth)
    copies = [pltpu.make_async_copy(w_ref.at[here, :], out_ref, sem.at[0])]
    if t == 0:
        copies.append(pltpu.make_async_copy(mask_ref, raw_ref, sem.at[1]))
    for copy in copies:
        copy.start()
    for copy in copies:
        copy.wait()
    if t == 0:
        open_ref[...] = raw_ref[...].astype(jnp.float32).astype(jnp.bfloat16)


def hold(plan, t, w, *mask):
    depth, D = w.shape[0] // plan.L, w.shape[1]
    size = w.size * w.dtype.itemsize
    shapes = [jax.ShapeDtypeStruct((depth, D), w.dtype)] + [jax.ShapeDtypeStruct(m.shape, jnp.bfloat16) for m in mask]
    return pl.pallas_call(
        functools.partial(hold_body, plan, t),
        out_shape=shapes,
        in_specs=[HBM] * (1 + len(mask)),
        out_specs=[VMEM] * len(shapes),
        scratch_shapes=[pltpu.VMEM(m.shape, m.dtype) for m in mask] + [pltpu.SemaphoreType.DMA((2,))],
        compiler_params=pltpu.CompilerParams(vmem_limit_bytes=GRANT - size * (6 + t) // 4),
        cost_estimate=pl.CostEstimate(flops=1 << 20, bytes_accessed=0, transcendentals=0),
    )(w, *mask)


def project_body(plan, cols, w_ref, a_ref, *refs):
    H, R = plan.H, plan.rows
    h = lax.axis_index("head")
    part = R // H
    for n in range(w_ref.shape[1] // cols):
        at = slice(n * cols, (n + 1) * cols)
        d = jnp.dot(a_ref[...], w_ref[:, at], preferred_element_type=jnp.float32)
        if len(refs) == 1:
            refs[0][:, at] = d
            continue
        sum_ref, send_ref, own_ref, all_ref = refs
        all_ref[:, at] = sum_ref[:, at] + d
        own_ref[:, at] = all_ref[pl.ds(pl.multiple_of(h * part, part), part), at]
        for u in range(1, H):
            to = (h + u) % H
            send_ref[(u - 1) * part : u * part, at] = all_ref[pl.ds(pl.multiple_of(to * part, part), part), at].astype(
                jnp.bfloat16
            )


def project(plan, t, piece, w, total):
    H, R = plan.H, plan.rows
    depth, D = piece.shape[1], w.shape[1]
    part = R // H
    last = t == plan.L - 1
    if last:
        shapes = [
            jax.ShapeDtypeStruct(((H - 1) * part, D), jnp.bfloat16),
            jax.ShapeDtypeStruct((part, D), jnp.float32),
        ]
    else:
        shapes = [jax.ShapeDtypeStruct((R, D), jnp.float32)]
    args = [w, piece] + ([total] if last else [])
    return pl.pallas_call(
        functools.partial(project_body, plan, 512),
        out_shape=shapes,
        in_specs=[VMEM] * len(args),
        out_specs=[VMEM] * len(shapes),
        scratch_shapes=[pltpu.VMEM((R, D), jnp.float32)] if last else [],
        compiler_params=pltpu.CompilerParams(vmem_limit_bytes=6 << 20),
        cost_estimate=pl.CostEstimate(flops=2 * R * depth * D, bytes_accessed=0, transcendentals=0),
        name="project",
    )(*args)


def layer(plan, queries, keys, values, tile_mask, out_weight):
    L, H, R = plan.L, plan.H, plan.rows
    wide = plan.group * HD
    _, _, j = plan.split(lax.axis_index("seq"))

    kv_send, full_send = [], []
    for t in range(L):
        p = (j + t) % L
        k_p = lax.dynamic_slice(keys, (0, p * HD), (R, HD))
        v_p = lax.dynamic_slice(values, (0, p * HD), (R, HD))
        q_p = lax.dynamic_slice(queries, (0, p * wide), (R, wide))
        kv_send.append(jnp.concatenate([k_p, v_p], axis=1))
        full_send.append(jnp.concatenate([k_p, v_p, q_p], axis=1))
    first_weight, mask = hold(plan, 0, out_weight, tile_mask)
    weights = [first_weight]
    for t in range(1, L):
        weights += hold(plan, t, out_weight)

    kv = {}
    side = plan.side_pairs()
    own = {}
    for k in [0, *plan.far()]:
        for t in range(L):
            own[k, t] = lax.ppermute(kv_send[t] if k else full_send[t], BOTH, plan.out_pairs(k, t))
    q = [own[0, t] for t in range(L)]
    near = jnp.concatenate([own[0, t][:, : 2 * HD] for t in range(L)], axis=0)
    near_side = lax.ppermute(near, BOTH, side)
    for t in range(L):
        kv[(0, 0, 0), t] = near, t * R
        kv[(0, 1, 0), t] = near_side, t * R
    both = jnp.concatenate([near, near_side], axis=0)
    for u in range(1, H):
        got = lax.ppermute(both, "head", plan.head_pairs(u))
        for t in range(L):
            kv[(0, 0, u), t] = got, t * R
            kv[(0, 1, u), t] = got, (L + t) * R
    for k in plan.far():
        far = jnp.concatenate([own[k, t] for t in range(L)], axis=0)
        far_side = lax.ppermute(far, BOTH, side)
        for n, block in enumerate((far, far_side)):
            got = {u: lax.ppermute(block, "head", plan.head_pairs(u)) for u in range(1, H)}
            for u in range(H):
                for t in range(L):
                    kv[(k, n, u), t] = got[u] if u else block, t * R
    spans = [(k, n, u) for k in [0, *plan.far()] for n in range(2) for u in range(H)]
    pieces = []
    if len(spans) * L * R <= STAGE:
        laid, where = index_of(plan, spans, kv)
        for t in range(L):
            out, *more = attend_one(plan, spans, t, mask, q[t], laid, where)
            if where is not None:
                laid, where = more, None
            pieces.append(lax.ppermute(out, BOTH, plan.back_pairs(t)))
    else:
        outs = attend_staged(plan, spans, mask, q, kv)
        for t in range(L):
            pieces.append(lax.ppermute(outs[t], BOTH, plan.back_pairs(t)))
    total = None
    for t in range(L):
        res = project(plan, t, pieces[t], weights[t], total)
        total = res[0]
    send, mine = res
    part = R // H
    for u in range(1, H):
        got = lax.ppermute(send[(u - 1) * part : u * part], "head", [(c, (c + u) % H) for c in range(H)])
        mine = mine + got.astype(jnp.float32)
    return mine.astype(jnp.bfloat16)


def solution(mesh):
    def program(queries, keys, values, tile_mask, out_weight):
        groups = keys.shape[1] // mesh.shape["head"] // HD
        rows = queries.shape[0] // mesh.shape["seq"]
        plan = Plan(mesh, groups, queries.shape[1] // keys.shape[1], rows, tile_mask.shape[0])

        def body(*args):
            return layer(plan, *args)

        step = jax.shard_map(
            body,
            mesh=mesh,
            in_specs=(P("seq", "head"), P("seq", "head"), P("seq", "head"), P(), P("head", None)),
            out_specs=P(("seq", "head"), None),
            check_vma=False,
        )
        return step(queries, keys, values, tile_mask, out_weight)

    return program
```

time: 45.4 us -> 40.8 us (0.90)
  the two profiles are of different devices: /device:TPU:0 before, /device:TPU:17 now
where the time goes in v2:
time: 40.8 us; the launch traced here: 40.4 us
  starting transfers between devices  16.6 us (41%)
  Pallas kernels  10.3 us (25%)
  waiting for transfers between devices  9.85 us (24%)
  local copies, waits for them, and re-layouts  2.55 us (6%)
  other arithmetic  0.97 us (2%)
    ppermute x4, starting transfers between devices, layer(): lax.ppermute(kv_send[t] if k else full_send[t], BOTH, plan.out_pairs(k, t))  7.35 us
    ppermute x2, starting transfers between devices, layer(): pieces.append(lax.ppermute(out, BOTH, plan.back_pairs(t)))  6.01 us
    pallas_call x2, Pallas kernels, hold(): pl.pallas_call(functools.partial(hold_body, plan, t), out_shape=shapes, i...  4.41 us
    ppermute x4, waiting for transfers between devices, layer(): lax.ppermute(kv_send[t] if k else full_send[t], BOTH, plan.out_pairs(k, t))  4.06 us
    pallas_call x2, Pallas kernels, attend_one(): pl.pallas_call(functools.partial(piece_body, plan, spans, t, where, len(k...  4.04 us
    ppermute x1, waiting for transfers between devices, layer(): far_side = lax.ppermute(far, BOTH, side)  2.27 us
    ppermute x1, waiting for transfers between devices, layer(): lax.ppermute(send[(u - 1) * part:u * part], 'head', [(c, (c + u) % H) for...  1.9 us
    pallas_call x2, Pallas kernels, project(): pl.pallas_call(functools.partial(project_body, plan, 512), out_shape=shap...  1.8 us
  transfers between devices with their start and end apart: 12, of which 6 were waited for; matrix products, arithmetic and copies ran while one was open for 0% of the time, Pallas kernels for 18%

profile of v2, /device:TPU:17, one launch (start us, length us, event | category | flops | bytes accessed | tf_op | source)
XLA Modules:
  0.0 40.4 jit_solution(14825952701319714994)
XLA Ops:
  0.0 1.0 %constant_dynamic-slice_fusion = (bf16[128,512]{1,0:T(8,128)(2,1)S(1)}, bf16[128,512]{1,0:T(8,128)(2,1)S(1)}) fusion(bf16[128,1024]{1,0:T(8,128)(2,1)} %param.5, s32[]{:T(128)S(6)} %select_n.45, s32[]{:T(128)S(6)} %select_n.42), kind=kLoop, calls=%fused_computation.9 | loop fusion | bytes 524296 | tf_op jit(solution)/shard_map/dynamic_slice | solution.py:327
  1.0 0.8 %constant_dynamic-slice_fusion.1 = (bf16[128,128]{1,0:T(8,128)(2,1)S(1)}, bf16[128,128]{1,0:T(8,128)(2,1)S(1)}, bf16[128,128]{1,0:T(8,128)(2,1)S(1)}, bf16[128,128]{1,0:T(8,128)(2,1)S(1)}) fusion(bf16[128,256]{1,0:T(8,128)(2,1)} %param.7, s32[]{:T(128)S(6)} %select_n.44, s32[]{:T(128)S(6)} %select_n.41, bf16[128,256]{1,0:T(8,128)(2,1)} %param.6), kind=kLoop, calls=%fused_computation.10 | loop fusion | bytes 262152 | tf_op jit(solution)/shard_map/dynamic_slice | solution.py:326
  1.8 3.8 %collective-permute-start.1 = (bf16[128,768]{1,0:T(8,128)(2,1)S(1)}, bf16[128,768]{1,0:T(8,128)(2,1)S(1)}, u32[]{:S(2)}, u32[]{:S(2)}) collective-permute-start(bf16[128,768]{1,0:T(8,128)(2,1)S(1)} %pad_maximum_fusion.2), channel_id=1, source_target_pairs={{0,0},{1,8},{2,2},{3,10},{8,1},{9,9},{10,3},{11,11},{4,4},{5,12},{... | collective-permute-start | bytes 589832 | tf_op jit(solution)/shard_map/ppermute | solution.py:340
  5.6 1.0 %collective-permute-start = (bf16[128,768]{1,0:T(8,128)(2,1)S(1)}, bf16[128,768]{1,0:T(8,128)(2,1)S(1)}, u32[]{:S(2)}, u32[]{:S(2)}) collective-permute-start(bf16[128,768]{1,0:T(8,128)(2,1)S(1)} %pad_maximum_fusion.1), channel_id=1, source_target_pairs={{0,2},{1,10},{2,0},{3,8},{8,3},{9,11},{10,1},{11,9},{4,6},{5,14},{... | collective-permute-start | bytes 589832 | tf_op jit(solution)/shard_map/ppermute | solution.py:340
  6.7 1.3 %collective-permute-start.5 = (bf16[128,256]{1,0:T(8,128)(2,1)S(1)}, bf16[128,256]{1,0:T(8,128)(2,1)S(1)}, u32[]{:S(2)}, u32[]{:S(2)}) collective-permute-start(bf16[128,256]{1,0:T(8,128)(2,1)S(1)} %pad_maximum_fusion.5), channel_id=1, source_target_pairs={{0,18},{1,26},{2,16},{3,24},{8,19},{9,27},{10,17},{11,25},{4,22},{... | collective-permute-start | bytes 196616 | tf_op jit(solution)/shard_map/ppermute | solution.py:340
  8.0 1.3 %collective-permute-start.4 = (bf16[128,256]{1,0:T(8,128)(2,1)S(1)}, bf16[128,256]{1,0:T(8,128)(2,1)S(1)}, u32[]{:S(2)}, u32[]{:S(2)}) collective-permute-start(bf16[128,256]{1,0:T(8,128)(2,1)S(1)} %pad_maximum_fusion.4), channel_id=1, source_target_pairs={{0,16},{1,24},{2,18},{3,26},{8,17},{9,25},{10,19},{11,27},{4,20},{... | collective-permute-start | bytes 196616 | tf_op jit(solution)/shard_map/ppermute | solution.py:340
  9.3 0.0 collective-permute-done.1.q_ref
  9.3 3.0 %collective-permute-done.q_ref = bf16[128,768]{1,0:T(8,128)(2,1)S(1)} collective-permute-done((bf16[128,768]{1,0:T(8,128)(2,1)S(1)}, bf16[128,768]{1,0:T(8,128)(2,1)S(1)}, u32[]{:S(2)}, u32[]{:S(2)}) %collective-permute-start) | collective-permute-done | bytes 196640 | tf_op jit(solution)/shard_map/ppermute | solution.py:340
  12.3 1.3 %collective-permute-start.2 = (bf16[256,256]{1,0:T(8,128)(2,1)S(1)}, bf16[256,256]{1,0:T(8,128)(2,1)S(1)}, u32[]{:S(2)}, u32[]{:S(2)}) collective-permute-start(bf16[256,256]{1,0:T(8,128)(2,1)S(1)} %pad_maximum_fusion.3.refs_0_), channel_id=1, source_target_pairs={{4,0},{5,1},{6,2},{7,3},{12,8},{13,9},{14,10},{15,11},{0,4},{1,5},... | collective-permute-start | bytes 393224 | tf_op jit(solution)/shard_map/ppermute | solution.py:343
  13.6 1.1 %collective-permute-done.4 = bf16[128,256]{1,0:T(8,128)(2,1)S(1)} collective-permute-done((bf16[128,256]{1,0:T(8,128)(2,1)S(1)}, bf16[128,256]{1,0:T(8,128)(2,1)S(1)}, u32[]{:S(2)}, u32[]{:S(2)}) %collective-permute-start.4) | collective-permute-done | bytes 65568 | tf_op jit(solution)/shard_map/ppermute | solution.py:340
  14.7 0.0 collective-permute-done.5
  14.7 1.3 %collective-permute-start.7 = (bf16[256,256]{1,0:T(8,128)(2,1)S(1)}, bf16[256,256]{1,0:T(8,128)(2,1)S(1)}, u32[]{:S(2)}, u32[]{:S(2)}) collective-permute-start(bf16[256,256]{1,0:T(8,128)(2,1)S(1)} %constant_dynamic-update-slice_fusion.refs_3_), channel_id=1, source_target_pairs={{4,0},{5,1},{6,2},{7,3},{12,8},{13,9},{14,10},{15,11},{0,4},{1,5},... | collective-permute-start | bytes 393224 | tf_op jit(solution)/shard_map/ppermute | solution.py:355
  16.0 0.2 collective-permute-done.2.refs_2_
  16.2 0.1 collective-permute-start.3
  16.3 0.5 %collective-permute-start.6 = (bf16[256,256]{1,0:T(8,128)(2,1)S(1)}, bf16[256,256]{1,0:T(8,128)(2,1)S(1)}, u32[]{:S(2)}, u32[]{:S(2)}) collective-permute-start(bf16[256,256]{1,0:T(8,128)(2,1)S(1)} %constant_dynamic-update-slice_fusion.refs_3_), channel_id=1, source_target_pairs={{1,0},{0,1},{3,2},{2,3},{5,4},{4,5},{7,6},{6,7},{9,8},{8,9},{11,10... | collective-permute-start | bytes 393224 | tf_op jit(solution)/shard_map/ppermute | solution.py:357
  16.8 2.3 %collective-permute-done.7.refs_5_ = bf16[256,256]{1,0:T(8,128)(2,1)S(1)} collective-permute-done((bf16[256,256]{1,0:T(8,128)(2,1)S(1)}, bf16[256,256]{1,0:T(8,128)(2,1)S(1)}, u32[]{:S(2)}, u32[]{:S(2)}) %collective-permute-start.7) | collective-permute-done | bytes 131104 | tf_op jit(solution)/shard_map/ppermute | solution.py:355
  19.1 0.0 collective-permute-start.8
  19.1 0.0 copy-start
  19.1 0.7 %copy-done = s32[32,32]{1,0:T(8,128)S(1)} copy-done((s32[32,32]{1,0:T(8,128)S(1)}, s32[32,32]{1,0:T(8,128)}, u32[]{:S(2)}) %copy-start) | copy-done | bytes 4120
  19.8 2.2 %shard_map.56 = (bf16[512,4096]{1,0:T(8,128)(2,1)S(1)}, bf16[32,32]{1,0:T(8,128)(2,1)S(1)}) custom-call(bf16[1024,4096]{1,0:T(8,128)(2,1)} %w_ref.3, s32[32,32]{1,0:T(8,128)S(1)} %copy-done), custom_call_target="tpu_custom_call" | custom-call | flops 1048576 | tf_op jit(solution)/shard_map/pallas_call | solution.py:261
  22.0 0.0 collective-permute-done.6.refs_4_
  22.0 0.0 collective-permute-done.8.refs_6_
  22.0 0.0 collective-permute-done.3.refs_1_
  22.0 2.1 %shard_map.57 = (bf16[128,512]{1,0:T(8,128)(2,1)S(1)}, bf16[2048,128]{1,0:T(8,128)(2,1)S(1)}, bf16[2048,256]{1,0:T(8,128)(2,1)S(1)}) custom-call(bf16[32,32]{1,0:T(8,128)(2,1)S(1)} %get-tuple-element.12.mask_ref, bf16[128,768]{1,0:T(8,128)(2,1)S(1)} %collective-permute-done.1.q_ref, bf16[256,256]{1,0:T(8,128)(2,1)S(1)} %pad_maximum_fusion.3.refs_0_, ...), custom_call_target="tpu_custom_call" | custom-call | flops 805306368 | tf_op jit(solution)/shard_map/pallas_call | solution.py:214
  24.1 5.0 %collective-permute-start.10 = (bf16[128,512]{1,0:T(8,128)(2,1)S(1)}, bf16[128,512]{1,0:T(8,128)(2,1)S(1)}, u32[]{:S(2)}, u32[]{:S(2)}) collective-permute-start(bf16[128,512]{1,0:T(8,128)(2,1)S(1)} %get-tuple-element.16), channel_id=1, source_target_pairs={{0,0},{8,1},{2,2},{10,3},{1,8},{9,9},{3,10},{11,11},{4,4},{12,5},{... | collective-permute-start | bytes 393224 | tf_op jit(solution)/shard_map/ppermute | solution.py:369
  29.2 2.0 %shard_map.58 = bf16[128,512]{1,0:T(8,128)(2,1)S(1)} custom-call(bf16[32,32]{1,0:T(8,128)(2,1)S(1)} %get-tuple-element.12.mask_ref, bf16[128,768]{1,0:T(8,128)(2,1)S(1)} %collective-permute-done.q_ref, bf16[2048,128]{1,0:T(8,128)(2,1)S(1)} %get-tuple-element.13.refs_0_, bf16[2048,256]{1,0:T(8,128)(2,1)S(1)} %get-tuple-element.14.refs_1_), custom_call_target="tpu_custom_call" | custom-call | flops 805306368 | tf_op jit(solution)/shard_map/pallas_call | solution.py:214
  31.1 1.0 %collective-permute-start.9 = (bf16[128,512]{1,0:T(8,128)(2,1)S(1)}, bf16[128,512]{1,0:T(8,128)(2,1)S(1)}, u32[]{:S(2)}, u32[]{:S(2)}) collective-permute-start(bf16[128,512]{1,0:T(8,128)(2,1)S(1)} %shard_map.58), channel_id=1, source_target_pairs={{2,0},{10,1},{0,2},{8,3},{3,8},{11,9},{1,10},{9,11},{6,4},{14,5},{... | collective-permute-start | bytes 393224 | tf_op jit(solution)/shard_map/ppermute | solution.py:369
  32.1 2.2 %shard_map.55.w_ref = bf16[512,4096]{1,0:T(8,128)(2,1)S(1)} custom-call(bf16[1024,4096]{1,0:T(8,128)(2,1)} %w_ref.3), custom_call_target="tpu_custom_call" | custom-call | flops 1048576 | tf_op jit(solution)/shard_map/pallas_call | solution.py:261
  34.3 0.0 collective-permute-done.10.a_ref
  34.3 0.7 %project.2.refs_0_ = f32[128,4096]{1,0:T(8,128)S(1)} custom-call(bf16[512,4096]{1,0:T(8,128)(2,1)S(1)} %get-tuple-element.15.w_ref, bf16[128,512]{1,0:T(8,128)(2,1)S(1)} %collective-permute-done.10.a_ref), custom_call_target="tpu_custom_call" | custom-call | flops 536870912 | tf_op jit(solution)/shard_map/project/pallas_call | solution.py:305
  35.1 1.4 %collective-permute-done.9.a_ref = bf16[128,512]{1,0:T(8,128)(2,1)S(1)} collective-permute-done((bf16[128,512]{1,0:T(8,128)(2,1)S(1)}, bf16[128,512]{1,0:T(8,128)(2,1)S(1)}, u32[]{:S(2)}, u32[]{:S(2)}) %collective-permute-start.9) | collective-permute-done | bytes 131104 | tf_op jit(solution)/shard_map/ppermute | solution.py:369
  36.5 1.1 %project.3 = (bf16[64,4096]{1,0:T(8,128)(2,1)S(1)}, f32[64,4096]{1,0:T(8,128)S(1)}) custom-call(bf16[512,4096]{1,0:T(8,128)(2,1)S(1)} %shard_map.55.w_ref, bf16[128,512]{1,0:T(8,128)(2,1)S(1)} %collective-permute-done.9.a_ref, f32[128,4096]{1,0:T(8,128)S(1)} %project.2.refs_0_), custom_call_target="tpu_custom_call" | custom-call | flops 536870912 | tf_op jit(solution)/shard_map/project/pallas_call | solution.py:305
  37.6 0.1 collective-permute-start.11
  37.7 1.9 %collective-permute-done.11 = bf16[64,4096]{1,0:T(8,128)(2,1)S(1)} collective-permute-done((bf16[64,4096]{1,0:T(8,128)(2,1)S(1)}, bf16[64,4096]{1,0:T(8,128)(2,1)S(1)}, u32[]{:S(2)}, u32[]{:S(2)}) %collective-permute-start.11) | collective-permute-done | bytes 524320 | tf_op jit(solution)/shard_map/ppermute | solution.py:381
  39.6 0.9 %add_convert_fusion = bf16[64,4096]{1,0:T(8,128)(2,1)} fusion(f32[64,4096]{1,0:T(8,128)S(1)} %get-tuple-element.17, bf16[64,4096]{1,0:T(8,128)(2,1)S(1)} %collective-permute-done.11), kind=kLoop, calls=%fused_computation | loop fusion | flops 786432 | bytes 2097152 | tf_op jit(solution)/shard_map/convert_element_type | solution.py:383
  (10 shorter events, 0.1 us)
Async XLA Ops:
  1.8 7.4 %collective-permute-start.1 = (bf16[128,768]{1,0:T(8,128)(2,1)S(1)}, bf16[128,768]{1,0:T(8,128)(2,1)S(1)}, u32[]{:S(2)}, u32[]{:S(2)}) collective-permute-start(bf16[128,768]{1,0:T(8,128)(2,1)S(1)} %pad_maximum_fusion.2), channel_id=1, source_target_pairs={{0,0},{1,8},{2,2},{3,10},{8,1},{9,9},{10,3},{11,11},{4,4},{5,12},{... | collective-permute-start | bytes 589832 | tf_op jit(solution)/shard_map/ppermute | solution.py:340
  5.6 6.7 %collective-permute-start = (bf16[128,768]{1,0:T(8,128)(2,1)S(1)}, bf16[128,768]{1,0:T(8,128)(2,1)S(1)}, u32[]{:S(2)}, u32[]{:S(2)}) collective-permute-start(bf16[128,768]{1,0:T(8,128)(2,1)S(1)} %pad_maximum_fusion.1), channel_id=1, source_target_pairs={{0,2},{1,10},{2,0},{3,8},{8,3},{9,11},{10,1},{11,9},{4,6},{5,14},{... | collective-permute-start | bytes 589832 | tf_op jit(solution)/shard_map/ppermute | solution.py:340
  6.7 8.0 %collective-permute-start.5 = (bf16[128,256]{1,0:T(8,128)(2,1)S(1)}, bf16[128,256]{1,0:T(8,128)(2,1)S(1)}, u32[]{:S(2)}, u32[]{:S(2)}) collective-permute-start(bf16[128,256]{1,0:T(8,128)(2,1)S(1)} %pad_maximum_fusion.5), channel_id=1, source_target_pairs={{0,18},{1,26},{2,16},{3,24},{8,19},{9,27},{10,17},{11,25},{4,22},{... | collective-permute-start | bytes 196616 | tf_op jit(solution)/shard_map/ppermute | solution.py:340
  8.0 6.7 %collective-permute-start.4 = (bf16[128,256]{1,0:T(8,128)(2,1)S(1)}, bf16[128,256]{1,0:T(8,128)(2,1)S(1)}, u32[]{:S(2)}, u32[]{:S(2)}) collective-permute-start(bf16[128,256]{1,0:T(8,128)(2,1)S(1)} %pad_maximum_fusion.4), channel_id=1, source_target_pairs={{0,16},{1,24},{2,18},{3,26},{8,17},{9,25},{10,19},{11,27},{4,20},{... | collective-permute-start | bytes 196616 | tf_op jit(solution)/shard_map/ppermute | solution.py:340
  12.3 3.9 %collective-permute-start.2 = (bf16[256,256]{1,0:T(8,128)(2,1)S(1)}, bf16[256,256]{1,0:T(8,128)(2,1)S(1)}, u32[]{:S(2)}, u32[]{:S(2)}) collective-permute-start(bf16[256,256]{1,0:T(8,128)(2,1)S(1)} %pad_maximum_fusion.3.refs_0_), channel_id=1, source_target_pairs={{4,0},{5,1},{6,2},{7,3},{12,8},{13,9},{14,10},{15,11},{0,4},{1,5},... | collective-permute-start | bytes 393224 | tf_op jit(solution)/shard_map/ppermute | solution.py:343
  14.7 4.4 %collective-permute-start.7 = (bf16[256,256]{1,0:T(8,128)(2,1)S(1)}, bf16[256,256]{1,0:T(8,128)(2,1)S(1)}, u32[]{:S(2)}, u32[]{:S(2)}) collective-permute-start(bf16[256,256]{1,0:T(8,128)(2,1)S(1)} %constant_dynamic-update-slice_fusion.refs_3_), channel_id=1, source_target_pairs={{4,0},{5,1},{6,2},{7,3},{12,8},{13,9},{14,10},{15,11},{0,4},{1,5},... | collective-permute-start | bytes 393224 | tf_op jit(solution)/shard_map/ppermute | solution.py:355
  16.2 5.8 %collective-permute-start.3 = (bf16[512,256]{1,0:T(8,128)(2,1)S(1)}, bf16[512,256]{1,0:T(8,128)(2,1)S(1)}, u32[]{:S(2)}, u32[]{:S(2)}) collective-permute-start(bf16[512,256]{1,0:T(8,128)(2,1)S(1)} %pad_maximum_fusion), channel_id=1, source_target_pairs={{1,0},{0,1},{3,2},{2,3},{5,4},{4,5},{7,6},{6,7},{9,8},{8,9},{11,10... | collective-permute-start | bytes 786440 | tf_op jit(solution)/shard_map/ppermute | solution.py:349
  16.3 5.7 %collective-permute-start.6 = (bf16[256,256]{1,0:T(8,128)(2,1)S(1)}, bf16[256,256]{1,0:T(8,128)(2,1)S(1)}, u32[]{:S(2)}, u32[]{:S(2)}) collective-permute-start(bf16[256,256]{1,0:T(8,128)(2,1)S(1)} %constant_dynamic-update-slice_fusion.refs_3_), channel_id=1, source_target_pairs={{1,0},{0,1},{3,2},{2,3},{5,4},{4,5},{7,6},{6,7},{9,8},{8,9},{11,10... | collective-permute-start | bytes 393224 | tf_op jit(solution)/shard_map/ppermute | solution.py:357
  19.1 3.0 %collective-permute-start.8 = (bf16[256,256]{1,0:T(8,128)(2,1)S(1)}, bf16[256,256]{1,0:T(8,128)(2,1)S(1)}, u32[]{:S(2)}, u32[]{:S(2)}) collective-permute-start(bf16[256,256]{1,0:T(8,128)(2,1)S(1)} %collective-permute-done.7.refs_5_), channel_id=1, source_target_pairs={{1,0},{0,1},{3,2},{2,3},{5,4},{4,5},{7,6},{6,7},{9,8},{8,9},{11,10... | collective-permute-start | bytes 393224 | tf_op jit(solution)/shard_map/ppermute | solution.py:357
  19.1 0.7 %copy-start = (s32[32,32]{1,0:T(8,128)S(1)}, s32[32,32]{1,0:T(8,128)}, u32[]{:S(2)}) copy-start(s32[32,32]{1,0:T(8,128)} %refs_0_.1) | copy-start | bytes 12292
  24.1 10.2 %collective-permute-start.10 = (bf16[128,512]{1,0:T(8,128)(2,1)S(1)}, bf16[128,512]{1,0:T(8,128)(2,1)S(1)}, u32[]{:S(2)}, u32[]{:S(2)}) collective-permute-start(bf16[128,512]{1,0:T(8,128)(2,1)S(1)} %get-tuple-element.16), channel_id=1, source_target_pairs={{0,0},{8,1},{2,2},{10,3},{1,8},{9,9},{3,10},{11,11},{4,4},{12,5},{... | collective-permute-start | bytes 393224 | tf_op jit(solution)/shard_map/ppermute | solution.py:369
  31.1 5.4 %collective-permute-start.9 = (bf16[128,512]{1,0:T(8,128)(2,1)S(1)}, bf16[128,512]{1,0:T(8,128)(2,1)S(1)}, u32[]{:S(2)}, u32[]{:S(2)}) collective-permute-start(bf16[128,512]{1,0:T(8,128)(2,1)S(1)} %shard_map.58), channel_id=1, source_target_pairs={{2,0},{10,1},{0,2},{8,3},{3,8},{11,9},{1,10},{9,11},{6,4},{14,5},{... | collective-permute-start | bytes 393224 | tf_op jit(solution)/shard_map/ppermute | solution.py:369
  37.6 2.0 %collective-permute-start.11 = (bf16[64,4096]{1,0:T(8,128)(2,1)S(1)}, bf16[64,4096]{1,0:T(8,128)(2,1)S(1)}, u32[]{:S(2)}, u32[]{:S(2)}) collective-permute-start(bf16[64,4096]{1,0:T(8,128)(2,1)S(1)} %get-tuple-element.18), channel_id=1, source_target_pairs={{0,1},{1,0},{2,3},{3,2},{4,5},{5,4},{6,7},{7,6},{8,9},{9,8},{10,11... | collective-permute-start | bytes 1572872 | tf_op jit(solution)/shard_map/ppermute | solution.py:381
